TPU v7x, 32 devices: a 4x4x1 block of a 4x4x8 slice. The times are simulated.
32 devices in a mesh: rep: 2 (over z, core), dp: 16 (over x, y).
Axes of the slice: x: 4, y: 4, z: 1, core: 2. Of those that a mesh axis runs over, the one named last changes fastest.
The devices are a block of a 4x4x8 slice.
Arguments:
- a: bfloat16 [32, 4, 4096, 512], P(('rep', 'dp')), parts along dimension 0
- g: bfloat16 [32, 4, 4096, 1792], P(('rep', 'dp')), parts along dimension 0
Outputs:
- output: bfloat16 [8, 512, 1792], P('rep'), parts along dimension 0
There are 2 independent parts. A program takes and returns all parts, laid end to end along the dimension named above; each array names one.
All inputs are finite; a program needn't handle non-finite values.
Results may differ from a plain program's by a relative error of at most 0.012.
Values are sent between devices in bfloat16 or wider.
A program may use at most 768 MiB of HBM per device.

v0:
```python
import jax
import jax.numpy as jnp


def solution(mesh):
    groups = mesh.shape["rep"]

    def step(a, g):
        a, g = (t.reshape(groups, -1, *t.shape[1:]) for t in (a, g))
        sums = jnp.einsum("rsntd,rsntf->rndf", a, g, preferred_element_type=jnp.float32)
        return sums.astype(jnp.bfloat16).reshape(-1, *sums.shape[2:])

    return step
```

profile of v0, /device:TPU:96, one launch (start us, length us, event | category | flops | bytes accessed | tf_op | source)
XLA Modules:
  0.0 362.0 jit_solution(15121877810708684009)
XLA Ops:
  0.0 40.0 %fusion.3 = f32[1,4,512,1792]{3,2,1,0:T(8,128)} fusion(bf16[1,4,4096,1792]{3,2,1,0:T(8,128)(2,1)} %param.1, bf16[1,4,4096,512]{3,2,1,0:T(8,128)(2,1)} %param), kind=kOutput, calls=%fused_computation.4 | convolution fusion | flops 30064771072 | bytes 90177536 | tf_op jit(solution)/rsntd,rsntf->rndf/dot_general | solution.py:10
  40.0 322.0 %all-reduce.2 = bf16[1,4,512,1792]{3,2,1,0:T(8,128)(2,1)} all-reduce(f32[1,4,512,1792]{3,2,1,0:T(8,128)} %fusion.3), channel_id=1, replica_groups=[2,16]<=[32], use_global_device_ids=true, to_apply=%add.clone | all-reduce | flops 3670016 | bytes 22020096 | tf_op jit(solution)/rsntd,rsntf->rndf/dot_general | solution.py:10
where the time goes:
time: 362 us
  blocking collectives  322 us (89%)
  matrix products  40 us (11%)
    dot_general x1, blocking collectives, step(): jnp.einsum('rsntd,rsntf->rndf', a, g, preferred_element_type=jnp.float32)  322 us
    dot_general x1, matrix products, step(): jnp.einsum('rsntd,rsntf->rndf', a, g, preferred_element_type=jnp.float32)  40 us

commit v1 on v0

v1 whole, which is shorter than its diff:
```python
import functools
import math

import jax
import jax.numpy as jnp
from jax import lax
from jax.experimental import pallas as pl
from jax.experimental.pallas import tpu as pltpu
from jax.sharding import PartitionSpec as P

MESH = pl.DeviceIdType.MESH
COLS = 256
LAGS = (3, 6, 9, 12, 15)
AG_LAGS = (2, 4)
RING = 8


def kernel(side, a_hbm, g_hbm, out, abuf, gbuf, acc, sb, r1, r2, acc2, sb2, r3, r4,
           asem, gsem, send, s1, s2, s3, s4, s5, s6, s7, s8):
    mats, _, rows = a_hbm.shape
    per = g_hbm.shape[2] // COLS
    units = mats * per
    slots = gbuf.shape[0]
    quarter = rows // side
    half = quarter // 2
    piece = quarter // side
    bit = piece // 2

    me = lax.axis_index("dp")
    x, y = me // side, me % side

    def place(u):
        f = u % 2
        s1_, s2_ = f + (1 - f) * side, f * side + (1 - f)
        p1, p2 = x * (1 - f) + y * f, y * (1 - f) + x * f

        def nbr(p, s, d):
            return me + ((p + d) % side - p) * s

        return ((p1, nbr(p1, s1_, 1), nbr(p1, s1_, side - 1)),
                (p2, nbr(p2, s2_, 1), nbr(p2, s2_, side - 1)))

    def put(src, dst, u, sem, to):
        pltpu.make_async_remote_copy(
            src_ref=src, dst_ref=dst, send_sem=send.at[u], recv_sem=sem.at[u],
            device_id={"dp": to}, device_id_type=MESH).start()

    def got(ref, u, sem):
        pltpu.make_async_remote_copy(
            src_ref=ref, dst_ref=ref, send_sem=send.at[u], recv_sem=sem.at[u],
            device_id={"dp": me}, device_id_type=MESH).wait_recv()

    def load_a(n):
        return pltpu.make_async_copy(a_hbm.at[n], abuf.at[n % 2], asem.at[n % 2])

    def load_g(u):
        return pltpu.make_async_copy(
            g_hbm.at[u // per, :, pl.ds(pl.multiple_of(u % per * COLS, COLS), COLS)],
            gbuf.at[u % slots], gsem.at[u % slots])

    def cut(start, size):
        return pl.ds(pl.multiple_of(start, bit), size)

    def cols(u):
        return pl.ds(pl.multiple_of(u % per * COLS, COLS), COLS)

    def scatter_first(u, p, plus, minus, src, near, far, big, small):
        (near_buf, near_sem), (far_buf, far_sem) = near, far
        opp, up, down = (p + 2) % side, (p + 1) % side, (p + side - 1) % side
        put(src.at[u, cut(opp * big, small)], far_buf.at[u, 0], u, far_sem, plus)
        put(src.at[u, cut(opp * big + small, small)], far_buf.at[u, 1], u, far_sem, minus)
        put(src.at[u, cut(up * big + small, small)], near_buf.at[u, 0, pl.ds(small, small)], u, near_sem, plus)
        put(src.at[u, cut(down * big, small)], near_buf.at[u, 1, pl.ds(0, small)], u, near_sem, minus)

    def scatter_second(u, p, plus, minus, total, src, near, far, big, small):
        (near_buf, near_sem), (far_buf, far_sem) = near, far
        up, down = (p + 1) % side, (p + side - 1) % side
        got(far_buf.at[u], u, far_sem)
        k = u % RING
        src[u, cut(up * big, small)] = (
            total[k, cut(up * big, small)] + far_buf[u, 0].astype(jnp.float32)).astype(src.dtype)
        src[u, cut(down * big + small, small)] = (
            total[k, cut(down * big + small, small)] + far_buf[u, 1].astype(jnp.float32)).astype(src.dtype)
        put(src.at[u, cut(up * big, small)], near_buf.at[u, 0, pl.ds(0, small)], u, near_sem, plus)
        put(src.at[u, cut(down * big + small, small)], near_buf.at[u, 1, pl.ds(small, small)], u, near_sem, minus)

    def compute(u):
        n = u // per

        @pl.when(u % per == 0)
        def _():
            load_a(n).wait()

            @pl.when(n + 1 < mats)
            def _():
                load_a(n + 1).start()

        load_g(u).wait()
        res = lax.dot_general(abuf[n % 2], gbuf[u % slots], (((0,), (0,)), ((), ())),
                              preferred_element_type=jnp.float32)
        acc[u % RING] = res
        sb[u] = res.astype(sb.dtype)

        @pl.when(u + slots < units)
        def _():
            load_g(u + slots).start()

        (p, plus, minus), _ = place(u)
        scatter_first(u, p, plus, minus, sb, (r2, s2), (r1, s1), quarter, half)

    def step1(u):
        (p, plus, minus), _ = place(u)
        scatter_second(u, p, plus, minus, acc, sb, (r2, s2), (r1, s1), quarter, half)

    def step2(u):
        (p1, _, _), (p, plus, minus) = place(u)
        got(r2.at[u], u, s2)
        k = u % RING
        t = acc[k, cut(p1 * quarter, quarter)] + r2[u, 0].astype(jnp.float32) + r2[u, 1].astype(jnp.float32)
        acc2[k] = t
        sb2[u] = t.astype(sb2.dtype)
        scatter_first(u, p, plus, minus, sb2, (r4, s4), (r3, s3), piece, bit)

    def step3(u):
        _, (p, plus, minus) = place(u)
        scatter_second(u, p, plus, minus, acc2, sb2, (r4, s4), (r3, s3), piece, bit)

    def mine(u, start, size):
        return out.at[u // per, cut(start, size), cols(u)]

    def step4(u):
        (p1, _, _), (p, plus, minus) = place(u)
        got(r4.at[u], u, s4)
        t = acc2[u % RING, cut(p * piece, piece)] + r4[u, 0].astype(jnp.float32) + r4[u, 1].astype(jnp.float32)
        at = p1 * quarter + p * piece
        out[u // per, cut(at, piece), cols(u)] = t.astype(out.dtype)
        put(mine(u, at, piece), mine(u, at, piece), u, s5, plus)
        put(mine(u, at, piece), mine(u, at, piece), u, s5, minus)

    def gather1(u):
        (p1, _, _), (p, plus, minus) = place(u)
        got(r2.at[u, 0, pl.ds(0, 2 * piece)], u, s5)
        at = p1 * quarter
        low, high = at + (p + side - 1) % side * piece, at + (p + 1) % side * piece + bit
        put(mine(u, low, bit), mine(u, low, bit), u, s6, plus)
        put(mine(u, high, bit), mine(u, high, bit), u, s6, minus)

    def gather2(u):
        (p, plus, minus), _ = place(u)
        got(r2.at[u, 0, pl.ds(0, piece)], u, s6)
        at = p * quarter
        put(mine(u, at, quarter), mine(u, at, quarter), u, s7, plus)
        put(mine(u, at, quarter), mine(u, at, quarter), u, s7, minus)

    def gather3(u):
        (p, plus, minus), _ = place(u)
        got(r2.at[u], u, s7)
        low, high = (p + side - 1) % side * quarter, (p + 1) % side * quarter + half
        put(mine(u, low, half), mine(u, low, half), u, s8, plus)
        put(mine(u, high, half), mine(u, high, half), u, s8, minus)

    def gather4(u):
        got(r2.at[u, 0], u, s8)

    def staged(t, lag, f):
        @pl.when((t >= lag) & (t < units + lag))
        def _():
            f(t - lag)

    load_a(0).start()
    for u in range(slots):
        load_g(u).start()

    barrier = pltpu.get_barrier_semaphore()
    for place_ in place(0):
        for to in place_[1:]:
            pl.semaphore_signal(barrier, inc=1, device_id={"dp": to}, device_id_type=MESH)
    pl.semaphore_wait(barrier, 4)

    @pl.loop(0, units + LAGS[-1])
    def _(t):
        staged(t, 0, compute)
        for lag, f in zip(LAGS, (step1, step2, step3, step4, gather1)):
            staged(t, lag, f)

    @pl.loop(0, units + AG_LAGS[-1])
    def _(t):
        staged(t, 0, gather2)
        for lag, f in zip(AG_LAGS, (gather3, gather4)):
            staged(t, lag, f)

    @pl.loop(0, units)
    def _(u):
        for ref, times in ((r2.at[u, 0], 6), (r4.at[u, 0], 6)):
            for _ in range(times):
                pltpu.make_async_remote_copy(
                    src_ref=ref, dst_ref=ref, send_sem=send.at[u], recv_sem=s1.at[u],
                    device_id={"dp": me}, device_id_type=MESH).wait_send()


def solution(mesh):
    side = math.isqrt(mesh.shape["dp"])

    def body(a, g):
        a, g = a[0], g[0]
        mats, tokens, rows = a.shape
        width = g.shape[2]
        units = mats * (width // COLS)
        quarter = rows // side
        piece = quarter // side
        bf16, f32 = jnp.bfloat16, jnp.float32
        dma = pltpu.SemaphoreType.DMA
        slots = 3
        return pl.pallas_call(
            functools.partial(kernel, side),
            out_shape=jax.ShapeDtypeStruct((mats, rows, width), bf16),
            in_specs=[pl.BlockSpec(memory_space=pl.ANY)] * 2,
            out_specs=pl.BlockSpec(memory_space=pltpu.VMEM),
            scratch_shapes=[
                pltpu.VMEM((2, tokens, rows), bf16),
                pltpu.VMEM((slots, tokens, COLS), bf16),
                pltpu.VMEM((RING, rows, COLS), f32),
                pltpu.VMEM((units, rows, COLS), bf16),
                pltpu.VMEM((units, 2, quarter // 2, COLS), bf16),
                pltpu.VMEM((units, 2, quarter, COLS), bf16),
                pltpu.VMEM((RING, quarter, COLS), f32),
                pltpu.VMEM((units, quarter, COLS), bf16),
                pltpu.VMEM((units, 2, piece // 2, COLS), bf16),
                pltpu.VMEM((units, 2, piece, COLS), bf16),
                dma((2,)), dma((slots,)), dma((units,)),
            ] + [dma((units,))] * 8,
            compiler_params=pltpu.CompilerParams(
                collective_id=0, has_side_effects=True, vmem_limit_bytes=56 << 20),
        )(a, g)

    return jax.shard_map(
        body, mesh=mesh, in_specs=(P(("rep", "dp")), P(("rep", "dp"))),
        out_specs=P("rep"), check_vma=False)
```

time: 362 us -> 134 us (0.37)
  blocking collectives: 322 us -> 0 us
  Pallas kernels: 0 us -> 127 us
  matrix products: 40 us -> 0 us
  local copies, waits for them, and re-layouts: 0 us -> 6.6 us
    dot_general x1 -> x0, blocking collectives: 322 us -> none  [step(): jnp.einsum('rsntd,rsntf->rndf', a, g, preferred_element_type=jnp.float32)]
    pallas_call x0 -> x1, Pallas kernels: none -> 127 us  [body(): pl.pallas_call(functools.partial(kernel, side), out_shape=jax.ShapeDtypeS...]
    dot_general x1 -> x0, matrix products: 40 us -> none  [step(): jnp.einsum('rsntd,rsntf->rndf', a, g, preferred_element_type=jnp.float32)]
    unnamed x0 -> x1, local copies, waits for them, and re-layouts: none -> 6.6 us
where the time goes in v1:
time: 134 us
  Pallas kernels  127 us (95%)
  local copies, waits for them, and re-layouts  6.6 us (5%)
    pallas_call x1, Pallas kernels, body(): pl.pallas_call(functools.partial(kernel, side), out_shape=jax.ShapeDtypeS...  127 us
    unnamed x1, local copies, waits for them, and re-layouts  6.6 us

profile of v1, /device:TPU:96, one launch (start us, length us, event | category | flops | bytes accessed | tf_op | source)
XLA Modules:
  0.0 134.0 jit_solution(17775545141885841120)
XLA Ops:
  0.0 127.4 %shard_map.28 = bf16[4,512,1792]{2,1,0:T(8,128)(2,1)} custom-call(bf16[4,4096,512]{2,1,0:T(8,128)(2,1)} %bitcast.3, bf16[4,4096,1792]{2,1,0:T(8,128)(2,1)} %bitcast.2), custom_call_target="tpu_custom_call" | custom-call | tf_op jit(solution)/shard_map/pallas_call | solution.py:214
  127.4 6.6 %copy.4 = bf16[4,512,1792]{2,1,0:T(8,128)(2,1)} copy(bf16[4,512,1792]{2,1,0:T(8,128)(2,1)} %shard_map.28) | data formatting | bytes 14680064

commit v2 on v0

v2 whole, which is shorter than its diff:
```python
import functools
import math

import jax
import jax.numpy as jnp
from jax import lax
from jax.experimental import pallas as pl
from jax.experimental.pallas import tpu as pltpu
from jax.sharding import PartitionSpec as P

MESH = pl.DeviceIdType.MESH
COLS = 256
LAGS = (3,6,9,12,15,19,30,45)
RING = 8
SLOTS = 4
CHUNKS = 4


def kernel(side, a_hbm, g_hbm, out, abuf, gbuf, acc, sb, r1, r2, acc2, sb2, r3, r4,
           first_sem, asem, gsem, send, *sems):
    s1, s2, s3, s4, s5, s6, s7, s8 = sems
    mats, tokens, rows = a_hbm.shape
    per = g_hbm.shape[2] // COLS
    units = mats * per
    quarter = rows // side
    half = quarter // 2
    piece = quarter // side
    bit = piece // 2

    me = lax.axis_index("dp")
    x, y = lax.div(me, side), lax.rem(me, side)

    def axis(p, stride):
        at = [lax.rem(p + d, side) for d in range(side)]
        return at, me + (at[1] - p) * stride, me + (at[side - 1] - p) * stride

    axes = (axis(x, side), axis(y, 1))
    order = ((axes[0], axes[1]), (axes[1], axes[0]))

    def put(src, dst, u, sem, to):
        pltpu.make_async_remote_copy(
            src_ref=src, dst_ref=dst, send_sem=send.at[u], recv_sem=sem.at[u],
            device_id={"dp": to}, device_id_type=MESH).start()

    def got(ref, u, sem):
        pltpu.make_async_remote_copy(
            src_ref=ref, dst_ref=ref, send_sem=send.at[u], recv_sem=sem.at[u],
            device_id={"dp": me}, device_id_type=MESH).wait_recv()

    def load_a(n):
        return pltpu.make_async_copy(a_hbm.at[n], abuf.at[lax.rem(n, 2)], asem.at[lax.rem(n, 2)])

    def cols(u, n):
        return pl.ds(pl.multiple_of((u - n * per) * COLS, COLS), COLS)

    def load_g(u):
        n = lax.div(u, per)
        at = cols(u, n)
        slot = lax.rem(u, SLOTS)
        return pltpu.make_async_copy(g_hbm.at[n, :, at], gbuf.at[slot], gsem.at[slot])

    def load_first(c):
        at = pl.ds(c * (tokens // CHUNKS), tokens // CHUNKS)
        return (pltpu.make_async_copy(a_hbm.at[0, at], abuf.at[0, at], first_sem.at[2 * c]),
                pltpu.make_async_copy(g_hbm.at[0, at, pl.ds(0, COLS)], gbuf.at[0, at], first_sem.at[2 * c + 1]))

    def cut(start, size):
        return pl.ds(pl.multiple_of(start, bit), size)

    def f32(v):
        return v.astype(jnp.float32)

    def first_sends(u, axis, src, near, near_sem, far, far_sem, big, small):
        at, plus, minus = axis
        opp, up, down = at[2] * big, at[1] * big, at[side - 1] * big
        put(src.at[u, cut(opp, small)], far.at[u, 0], u, far_sem, plus)
        put(src.at[u, cut(opp + small, small)], far.at[u, 1], u, far_sem, minus)
        put(src.at[u, cut(up + small, small)], near.at[u, 0, pl.ds(small, small)], u, near_sem, plus)
        put(src.at[u, cut(down, small)], near.at[u, 1, pl.ds(0, small)], u, near_sem, minus)

    def second_sends(u, axis, total, src, near, near_sem, far, far_sem, big, small):
        at, plus, minus = axis
        up, down = cut(at[1] * big, small), cut(at[side - 1] * big + small, small)
        k = lax.rem(u, RING)
        got(far.at[u], u, far_sem)
        src[u, up] = (total[k, up] + f32(far[u, 0])).astype(src.dtype)
        src[u, down] = (total[k, down] + f32(far[u, 1])).astype(src.dtype)
        put(src.at[u, up], near.at[u, 0, pl.ds(0, small)], u, near_sem, plus)
        put(src.at[u, down], near.at[u, 1, pl.ds(small, small)], u, near_sem, minus)

    def dot(lhs, rhs):
        return lax.dot_general(lhs, rhs, (((0,), (0,)), ((), ())), preferred_element_type=jnp.float32)

    def first_unit():
        for c in range(CHUNKS):
            at = pl.ds(c * (tokens // CHUNKS), tokens // CHUNKS)
            for copy in load_first(c):
                copy.wait()
            res = dot(abuf[0, at], gbuf[0, at])
            if c:
                res = res + acc[0]
            acc[0] = res
        sb[0] = res.astype(sb.dtype)
        first_sends(0, order[0][0], sb, r2, s2, r1, s1, quarter, half)

    def compute(u, f):
        n = lax.div(u, per)
        slot = lax.rem(u, SLOTS)

        @pl.when(u + 2 < units)
        def _():
            load_g(u + 2).start()

        @pl.when((u == n * per + 1) & (n + 1 < mats))
        def _():
            load_a(n + 1).start()

        load_g(u).wait()

        @pl.when(u == n * per)
        def _():
            load_a(n).wait()

        res = dot(abuf[lax.rem(n, 2)], gbuf[slot])
        acc[lax.rem(u, RING)] = res
        sb[u] = res.astype(sb.dtype)
        first_sends(u, order[f][0], sb, r2, s2, r1, s1, quarter, half)

    def step1(u, f):
        second_sends(u, order[f][0], acc, sb, r2, s2, r1, s1, quarter, half)

    def step2(u, f):
        own = cut(order[f][0][0][0] * quarter, quarter)
        k = lax.rem(u, RING)
        got(r2.at[u], u, s2)
        t = acc[k, own] + f32(r2[u, 0]) + f32(r2[u, 1])
        acc2[k] = t
        sb2[u] = t.astype(sb2.dtype)
        first_sends(u, order[f][1], sb2, r4, s4, r3, s3, piece, bit)

    def step3(u, f):
        second_sends(u, order[f][1], acc2, sb2, r4, s4, r3, s3, piece, bit)

    def pass_on(u, start, size, sem, to):
        n = lax.div(u, per)
        ref = out.at[n, cut(start, size), cols(u, n)]
        put(ref, ref, u, sem, to)

    def step4(u, f):
        (at1, _, _), (at2, plus, minus) = order[f]
        got(r4.at[u], u, s4)
        t = acc2[lax.rem(u, RING), cut(at2[0] * piece, piece)] + f32(r4[u, 0]) + f32(r4[u, 1])
        at = at1[0] * quarter + at2[0] * piece
        n = lax.div(u, per)
        out[n, cut(at, piece), cols(u, n)] = t.astype(out.dtype)
        pass_on(u, at, piece, s5, plus)
        pass_on(u, at, piece, s5, minus)

    def gather1(u, f):
        (at1, _, _), (at2, plus, minus) = order[f]
        got(r2.at[u, 0, pl.ds(0, 2 * piece)], u, s5)
        pass_on(u, at1[0] * quarter + at2[side - 1] * piece, bit, s6, plus)
        pass_on(u, at1[0] * quarter + at2[1] * piece + bit, bit, s6, minus)

    def gather2(u, f):
        at, plus, minus = order[f][0]
        got(r2.at[u, 0, pl.ds(0, piece)], u, s6)
        pass_on(u, at[0] * quarter, quarter, s7, plus)
        pass_on(u, at[0] * quarter, quarter, s7, minus)

    def gather3(u, f):
        at, plus, minus = order[f][0]
        got(r2.at[u], u, s7)
        pass_on(u, at[side - 1] * quarter, half, s8, plus)
        pass_on(u, at[1] * quarter + half, half, s8, minus)

    def gather4(u, f):
        got(r2.at[u, 0], u, s8)
        for ref, times in ((r2.at[u], 3), (r4.at[u], 3)):
            for _ in range(times):
                pltpu.make_async_remote_copy(
                    src_ref=ref, dst_ref=ref, send_sem=send.at[u], recv_sem=s1.at[u],
                    device_id={"dp": me}, device_id_type=MESH).wait_send()

    for c in range(CHUNKS):
        for copy in load_first(c):
            copy.start()
    load_g(1).start()

    barrier = pltpu.get_barrier_semaphore()
    for _, plus, minus in axes:
        for to in (plus, minus):
            pl.semaphore_signal(barrier, inc=1, device_id={"dp": to}, device_id_type=MESH)
    pl.semaphore_wait(barrier, 4)

    load_g(2).start()
    first_unit()
    stages = (compute, step1, step2, step3, step4, gather1, gather2, gather3, gather4)
    steps = units + LAGS[-1]

    @pl.loop(0, (steps + 1) // 2)
    def _(v):
        for k in range(2):
            for lag, stage in zip((0,) + LAGS, stages):
                u = 2 * v + (k - lag)

                @pl.when((u >= (1 if stage is compute else 0)) & (u < units))
                def _():
                    stage(u, (k - lag) % 2)


def solution(mesh):
    side = math.isqrt(mesh.shape["dp"])

    def body(a, g):
        a, g = a[0], g[0]
        mats, tokens, rows = a.shape
        width = g.shape[2]
        per = width // COLS
        units = mats * per
        quarter = rows // side
        piece = quarter // side
        bf16, f32 = jnp.bfloat16, jnp.float32
        dma = pltpu.SemaphoreType.DMA
        return pl.pallas_call(
            functools.partial(kernel, side),
            out_shape=pltpu.VMEM((mats, rows, width), bf16),
            in_specs=[pl.BlockSpec(memory_space=pl.ANY)] * 2,
            out_specs=pl.BlockSpec(memory_space=pltpu.VMEM),
            scratch_shapes=[
                pltpu.VMEM((2, tokens, rows), bf16),
                pltpu.VMEM((SLOTS, tokens, COLS), bf16),
                pltpu.VMEM((RING, rows, COLS), f32),
                pltpu.VMEM((units, rows, COLS), bf16),
                pltpu.VMEM((units, 2, quarter // 2, COLS), bf16),
                pltpu.VMEM((units, 2, quarter, COLS), bf16),
                pltpu.VMEM((RING, quarter, COLS), f32),
                pltpu.VMEM((units, quarter, COLS), bf16),
                pltpu.VMEM((units, 2, piece // 2, COLS), bf16),
                pltpu.VMEM((units, 2, piece, COLS), bf16),
                dma((2 * CHUNKS,)), dma((2,)), dma((SLOTS,)),
            ] + [dma((units,))] * 9,
            compiler_params=pltpu.CompilerParams(
                collective_id=0, has_side_effects=True, vmem_limit_bytes=42 << 20),
        )(a, g)

    return jax.shard_map(
        body, mesh=mesh, in_specs=(P(("rep", "dp")), P(("rep", "dp"))),
        out_specs=P("rep"), check_vma=False)
```

time: 362 us -> 98 us (0.27)
  blocking collectives: 322 us -> 0 us
  Pallas kernels: 0 us -> 94.4 us
  matrix products: 40 us -> 0 us
    dot_general x1 -> x0, blocking collectives: 322 us -> none  [step(): jnp.einsum('rsntd,rsntf->rndf', a, g, preferred_element_type=jnp.float32)]
    pallas_call x0 -> x1, Pallas kernels: none -> 94.4 us  [body(): pl.pallas_call(functools.partial(kernel, side), out_shape=pltpu.VMEM((mat...]
    dot_general x1 -> x0, matrix products: 40 us -> none  [step(): jnp.einsum('rsntd,rsntf->rndf', a, g, preferred_element_type=jnp.float32)]
where the time goes in v2:
time: 98 us; the launch traced here: 97.5 us
  Pallas kernels  94.4 us (96%)
  local copies, waits for them, and re-layouts  3.05 us (3%)
    pallas_call x1, Pallas kernels, body(): pl.pallas_call(functools.partial(kernel, side), out_shape=pltpu.VMEM((mat...  94.4 us
    unnamed x1, local copies, waits for them, and re-layouts  3.05 us

profile of v2, /device:TPU:96, one launch (start us, length us, event | category | flops | bytes accessed | tf_op | source)
XLA Modules:
  0.0 97.5 jit_solution(14669156396555609016)
XLA Ops:
  0.0 94.4 %shard_map.28 = bf16[4,512,1792]{2,1,0:T(8,128)(2,1)S(1)} custom-call(bf16[4,4096,512]{2,1,0:T(8,128)(2,1)} %bitcast.3, bf16[4,4096,1792]{2,1,0:T(8,128)(2,1)} %bitcast.2), custom_call_target="tpu_custom_call" | custom-call | tf_op jit(solution)/shard_map/pallas_call | solution.py:225
  94.4 3.1 %copy.4 = bf16[4,512,1792]{2,1,0:T(8,128)(2,1)} copy(bf16[4,512,1792]{2,1,0:T(8,128)(2,1)S(1)} %shard_map.28) | data formatting | bytes 14680064
